TPU v7x, 32 devices: a whole 2x2x4 slice. The times are simulated.
32 devices in a mesh: fsdp: 8 (over z, y), tp: 4 (over x, core).
Axes of the slice: x: 2, y: 2, z: 4, core: 2. Of those that a mesh axis runs over, the one named last changes fastest.
Arguments:
- base_o: bfloat16 [2, 8192, 8192], P(None, 'tp', 'fsdp'), may hold values from -0.0625 to 0.0625
- base_down: bfloat16 [2, 28672, 8192], P(None, 'tp', 'fsdp'), may hold values from -0.03125 to 0.03125
- factor_a_o: bfloat16 [2, 64, 4, 2048], P(None, None, None, 'fsdp'), may hold values from -0.0625 to 0.0625
- factor_b_o: bfloat16 [2, 8192, 64], P(None, 'fsdp'), may hold values from -1.1953125 to 1.1953125
- factor_a_down: bfloat16 [2, 64, 4, 7168], P(None, None, None, 'fsdp'), may hold values from -0.03125 to 0.03125
- factor_b_down: bfloat16 [2, 8192, 64], P(None, 'fsdp'), may hold values from -1.1953125 to 1.1953125
- magnitude_o: float32 [2, 8192], P(None, 'fsdp'), may hold values from 30 to 300
- magnitude_down: float32 [2, 8192], P(None, 'fsdp'), may hold values from 30 to 300
Outputs:
- merged_o: bfloat16 [2, 8192, 8192], P(None, 'tp', 'fsdp')
- merged_down: bfloat16 [2, 28672, 8192], P(None, 'tp', 'fsdp')
All inputs are finite; a program needn't handle non-finite values.
Results may differ from a plain program's by a relative error of at most 0.001.
Values may be sent and summed in bfloat16 or wider, within the bound.
A program may use at most 192 MiB of HBM per device.

v0:
```python
import functools

import jax
import jax.numpy as jnp
from jax import lax
from jax.experimental import pallas as pl
from jax.experimental.pallas import tpu as pltpu
from jax.sharding import PartitionSpec as P

MESH = pl.DeviceIdType.MESH
F32 = jnp.float32
BF16 = jnp.bfloat16


def row_tile(rows, most):
    return max(t for t in range(16, most + 1, 16) if rows % t == 0)


def gather_kernel(
    n,
    n_tp,
    sizes,
    rank,
    base_o,
    base_d,
    a_o,
    a_d,
    b_o,
    b_d,
    mag_o,
    mag_d,
    held_o,
    held_d,
    full_a,
    weights,
    scale,
    block,
    acc,
    sums,
    peers,
    read_sem,
    own_sem,
    send_sem,
    recv_sem,
    sum_send,
    sum_recv,
):
    layers, columns = mag_o.shape
    depth = n // 2
    me, t = lax.axis_index("fsdp"), lax.axis_index("tp")
    z, y = me // 2, me % 2
    other = z * 2 + 1 - y
    has_lo, has_hi = z > 0, z < depth - 1

    def to_fsdp(f):
        return {"fsdp": f}

    barrier = pltpu.get_barrier_semaphore()

    def greet(device):
        pl.semaphore_signal(barrier, inc=1, device_id=device, device_id_type=MESH)

    greet(to_fsdp(other))
    for k in range(1, n_tp):
        greet({"tp": (t + k) % n_tp})
    pl.when(has_lo)(lambda: greet(to_fsdp(me - 2)))
    pl.when(has_hi)(lambda: greet(to_fsdp(me + 2)))

    def slot_of(e, lo, side):
        return (z - e if lo else z + e) * 2 + side

    bases = (base_o, base_d)
    helds = (held_o, held_d)
    starts = (0, sizes[0])

    def read(p, layer, f):
        rows = pl.ds(pl.multiple_of(f * sizes[p], 16), sizes[p])
        return pltpu.make_async_copy(
            bases[p].at[layer, rows], helds[p].at[layer, rows], read_sem.at[p, layer, f]
        )

    def read_slot(f):
        for p in range(2):
            for layer in range(layers):
                read(p, layer, f).start()

    read_slot(me)
    read_slot(other)

    @pl.loop(1, depth)
    def _(d):
        for side in (y, 1 - y):
            pl.when(z - d >= 0)(lambda: read_slot(slot_of(d, True, side)))
            pl.when(z + d < depth)(lambda: read_slot(slot_of(d, False, side)))

    for p, a in enumerate((a_o, a_d)):
        parts = []
        for layer in range(layers):
            rows = a[layer, :, 0, :].astype(F32)
            for u in range(1, n_tp):
                rows = jnp.where(t == u, a[layer, :, u, :].astype(F32), rows)
            parts.append(rows)
        block[pl.ds(starts[p], sizes[p]), :] = jnp.concatenate(parts, axis=0).T.astype(BF16)

    ends = has_lo.astype(jnp.int32) + has_hi.astype(jnp.int32)
    pl.semaphore_wait(barrier, n_tp + ends)

    def send(source, f, way, target):
        return pltpu.make_async_remote_copy(
            src_ref=source,
            dst_ref=full_a.at[f],
            send_sem=send_sem.at[way, f],
            recv_sem=recv_sem.at[f],
            device_id=to_fsdp(target),
            device_id_type=MESH,
        )

    def arrived(f):
        send(full_a.at[f], f, 0, other).wait_recv()

    pl.when(has_lo)(lambda: send(block, me, 1, me - 2).start())
    pl.when(has_hi)(lambda: send(block, me, 2, me + 2).start())
    send(block, me, 0, other).start()
    own = pltpu.make_async_copy(block, full_a.at[me], own_sem)
    own.start()

    for p, b in enumerate((b_o, b_d)):
        for layer in range(layers):
            weights[p, layer] = jnp.zeros((layers * rank, columns), BF16)
            weights[p, layer, pl.ds(layer * rank, rank), :] = (
                b[layer].astype(F32) * 0.25
            ).astype(BF16)
    acc[...] = jnp.zeros_like(acc)
    own.wait()

    wide = 256 if columns % 256 == 0 else columns

    def process(f):
        for p in range(2):
            tile = row_tile(sizes[p], 256)

            @pl.loop(0, layers)
            def _(layer):
                read(p, layer, f).wait()

                @pl.loop(0, sizes[p] // tile)
                def _(i):
                    rows = pl.ds(pl.multiple_of(starts[p] + i * tile, 16), tile)
                    held = pl.ds(pl.multiple_of(f * sizes[p] + i * tile, 16), tile)
                    left = full_a[f, rows, :]
                    for c in range(0, columns, wide):
                        cut = pl.ds(c, wide)
                        total = jnp.dot(
                            left, weights[p, layer, :, cut], preferred_element_type=F32
                        ) + helds[p][layer, held, cut].astype(F32)
                        acc[p, layer, :, cut] += jnp.sum(
                            (total * total).reshape(tile // 8, 8, wide), axis=0
                        )

    def from_other(e):
        def take(f):
            arrived(f)
            process(f)

        pl.when(z - e >= 0)(lambda: take(slot_of(e, True, 1 - y)))
        pl.when((e > 0) & (z + e < depth))(lambda: take(slot_of(e, False, 1 - y)))

    process(me)

    @pl.loop(1, depth)
    def _(d):
        @pl.when(z - d >= 0)
        def _():
            f = slot_of(d, True, y)
            arrived(f)
            pl.when(has_hi)(lambda: send(full_a.at[f], f, 2, me + 2).start())
            send(full_a.at[f], f, 0, other).start()

        @pl.when(z + d < depth)
        def _():
            f = slot_of(d, False, y)
            arrived(f)
            pl.when(has_lo)(lambda: send(full_a.at[f], f, 1, me - 2).start())
            send(full_a.at[f], f, 0, other).start()

        from_other(d - 1)
        pl.when(z - d >= 0)(lambda: process(slot_of(d, True, y)))
        pl.when(z + d < depth)(lambda: process(slot_of(d, False, y)))

    from_other(jnp.int32(depth - 1))

    for p in range(2):
        for layer in range(layers):
            sums[p * layers + layer, :] = jnp.sum(acc[p, layer], axis=0)

    pl.when(has_lo)(lambda: send(block, me, 1, me - 2).wait_send())
    pl.when(has_hi)(lambda: send(block, me, 2, me + 2).wait_send())
    send(block, me, 0, other).wait_send()

    @pl.loop(1, depth)
    def _(d):
        @pl.when(z - d >= 0)
        def _():
            f = slot_of(d, True, y)
            pl.when(has_hi)(lambda: send(full_a.at[f], f, 2, me + 2).wait_send())
            send(full_a.at[f], f, 0, other).wait_send()

        @pl.when(z + d < depth)
        def _():
            f = slot_of(d, False, y)
            pl.when(has_lo)(lambda: send(full_a.at[f], f, 1, me - 2).wait_send())
            send(full_a.at[f], f, 0, other).wait_send()

    def share(k):
        return pltpu.make_async_remote_copy(
            src_ref=sums,
            dst_ref=peers.at[k - 1],
            send_sem=sum_send.at[k - 1],
            recv_sem=sum_recv.at[k - 1],
            device_id={"tp": (t + k) % n_tp},
            device_id_type=MESH,
        )

    for k in range(1, n_tp):
        share(k).start()
    square = sums[...]
    for k in range(1, n_tp):
        share(k).wait()
    for k in range(1, n_tp):
        square = square + peers[k - 1]
    magnitude = jnp.concatenate([mag_o[...], mag_d[...]], axis=0)
    scale[...] = magnitude * lax.rsqrt(square + 1e-06)


def finish_kernel(sizes, held_o, held_d, full_a, weights, scale, out_o, out_d):
    layers, _, columns = held_o.shape
    layer, f = pl.program_id(0), pl.program_id(1)
    wide = 256 if columns % 256 == 0 else columns
    for p, (held, out) in enumerate(((held_o, out_o), (held_d, out_d))):
        size, start = sizes[p], sum(sizes[:p])
        tile = row_tile(size, 256)
        factor = scale[pl.ds(p * layers + layer, 1), :]

        @pl.loop(0, size // tile)
        def _(i):
            rows = pl.ds(pl.multiple_of(start + i * tile, 16), tile)
            inside = pl.ds(pl.multiple_of(f * size + i * tile, 16), tile)
            here = pl.ds(pl.multiple_of(i * tile, 16), tile)
            left = full_a[f, rows, :]
            for c in range(0, columns, wide):
                cut = pl.ds(c, wide)
                total = jnp.dot(
                    left, weights[p, layer, :, cut], preferred_element_type=F32
                ) + held[layer, inside, cut].astype(F32)
                out[0, here, cut] = (total * factor[:, c : c + wide]).astype(BF16)


def solution(mesh):
    n, n_tp = mesh.shape["fsdp"], mesh.shape["tp"]
    in_vmem = pl.BlockSpec(memory_space=pltpu.VMEM)
    anywhere = pl.BlockSpec(memory_space=pl.ANY)

    def local(base_o, base_d, a_o, b_o, a_d, b_d, mag_o, mag_d):
        layers, rank, _, part_o = a_o.shape
        sizes = (part_o, a_d.shape[3])
        columns = base_o.shape[2]
        depth = layers * rank
        base_o = pltpu.with_memory_space_constraint(base_o, pltpu.HBM)
        base_d = pltpu.with_memory_space_constraint(base_d, pltpu.HBM)
        shapes = (
            pltpu.VMEM(base_o.shape, BF16),
            pltpu.VMEM(base_d.shape, BF16),
            pltpu.VMEM((n, sum(sizes), depth), BF16),
            pltpu.VMEM((2, layers, depth, columns), BF16),
            pltpu.VMEM((2 * layers, columns), F32),
        )
        held_o, held_d, full_a, weights, scale = pl.pallas_call(
            functools.partial(gather_kernel, n, n_tp, sizes, rank),
            out_shape=shapes,
            in_specs=[anywhere] * 2 + [in_vmem] * 6,
            out_specs=[in_vmem] * 5,
            scratch_shapes=[
                pltpu.VMEM((sum(sizes), depth), BF16),
                pltpu.VMEM((2, layers, 8, columns), F32),
                pltpu.VMEM((2 * layers, columns), F32),
                pltpu.VMEM((n_tp - 1, 2 * layers, columns), F32),
                pltpu.SemaphoreType.DMA((2, layers, n)),
                pltpu.SemaphoreType.DMA,
                pltpu.SemaphoreType.DMA((3, n)),
                pltpu.SemaphoreType.DMA((n,)),
                pltpu.SemaphoreType.DMA((n_tp - 1,)),
                pltpu.SemaphoreType.DMA((n_tp - 1,)),
            ],
            compiler_params=pltpu.CompilerParams(
                collective_id=0, has_side_effects=True, vmem_limit_bytes=20 << 20
            ),
            name="gather_squares",
        )(
            base_o, base_d, a_o, a_d, b_o.swapaxes(1, 2), b_d.swapaxes(1, 2), mag_o, mag_d
        )

        kept = [
            pltpu.with_memory_space_constraint(x, pltpu.VMEM)
            for x in (held_o, held_d, full_a, weights, scale)
        ]
        return pl.pallas_call(
            functools.partial(finish_kernel, sizes),
            out_shape=[jax.ShapeDtypeStruct(b.shape, BF16) for b in (base_o, base_d)],
            grid=(layers, n),
            in_specs=[in_vmem] * 5,
            out_specs=[
                pl.BlockSpec((1, size, columns), lambda i, f: (i, f, 0)) for size in sizes
            ],
            compiler_params=pltpu.CompilerParams(vmem_limit_bytes=20 << 20),
            name="finish",
        )(*kept)

    return jax.shard_map(
        local,
        mesh=mesh,
        in_specs=(
            P(None, "tp", "fsdp"),
            P(None, "tp", "fsdp"),
            P(None, None, None, "fsdp"),
            P(None, "fsdp", None),
            P(None, None, None, "fsdp"),
            P(None, "fsdp", None),
            P(None, "fsdp"),
            P(None, "fsdp"),
        ),
        out_specs=(P(None, "tp", "fsdp"), P(None, "tp", "fsdp")),
        check_vma=False,
    )
```

profile of v0, /device:TPU:0, one launch (start us, length us, event | category | flops | bytes accessed | tf_op | source)
XLA Modules:
  0.0 66.7 jit_solution(10906402798715115822)
XLA Ops:
  0.6 42.5 %gather_squares.1 = (bf16[2,2048,1024]{2,1,0:T(8,128)(2,1)S(1)}, bf16[2,7168,1024]{2,1,0:T(8,128)(2,1)S(1)}, bf16[8,1152,128]{2,1,0:T(8,128)(2,1)S(1)}, bf16[2,2...) custom-call(bf16[2,2048,1024]{2,1,0:T(8,128)(2,1)} %base_o.1, bf16[2,7168,1024]{2,1,0:T(8,128)(2,1)} %base_d.1, ...), custom_call_target="tpu_custom_call" | custom-call | tf_op jit(solution)/shard_map/gather_squares/pallas_call | solution.py:277
  43.2 23.5 %finish.1 = (bf16[2,2048,1024]{2,1,0:T(8,128)(2,1)}, bf16[2,7168,1024]{2,1,0:T(8,128)(2,1)}) custom-call(bf16[2,2048,1024]{2,1,0:T(8,128)(2,1)S(1)} %get-tuple-element.7.held_o, bf16[2,7168,1024]{2,1,0:T(8,128)(2,1)S(1)} %get-tuple-element.8.held_d, bf16[8,1152,128]{2,1,0:T(8,128)(2,1)S(1)} %get-tuple-element.9.full_a, ...), custom_call_target="tpu_custom_call" | custom-call | tf_op jit(solution)/shard_map/finish/pallas_call | solution.py:306
where the time goes:
time: 66.8 us; the launch traced here: 66.7 us
  Pallas kernels  66 us (99%)
    pallas_call x1, Pallas kernels, local(): pl.pallas_call(functools.partial(gather_kernel, n, n_tp, sizes, rank), ou...  42.5 us
    pallas_call x1, Pallas kernels, local(): pl.pallas_call(functools.partial(finish_kernel, sizes), out_shape=[jax.Sh...  23.5 us

commit v1 on v0

v1 whole, which is shorter than its diff:
```python
import functools

import jax
import jax.numpy as jnp
from jax import lax
from jax.experimental import pallas as pl
from jax.experimental.pallas import tpu as pltpu
from jax.sharding import PartitionSpec as P

MESH = pl.DeviceIdType.MESH
F32 = jnp.float32
BF16 = jnp.bfloat16


def pieces_of(sizes, most):
    found = []
    for p, size in enumerate(sizes):
        rows = max(t for t in range(16, most + 1, 16) if size % t == 0)
        found += [(p, k * rows, rows) for k in range(size // rows)]
    return found


def gather_kernel(
    n,
    n_tp,
    sizes,
    rank,
    base_o,
    base_d,
    a_o,
    a_d,
    b_o,
    b_d,
    mag_o,
    mag_d,
    held_o,
    held_d,
    full_a,
    weights,
    scale,
    block,
    acc,
    sums,
    peers,
    read_sem,
    send_sem,
    recv_sem,
    sum_send,
    sum_recv,
):
    layers, columns = mag_o.shape
    depth = n // 2
    me, t = lax.axis_index("fsdp"), lax.axis_index("tp")
    z, y = me // 2, me % 2
    other = z * 2 + 1 - y
    has_lo, has_hi = z > 0, z < depth - 1
    starts = (0, sizes[0])
    pieces = pieces_of(sizes, 448)
    count = len(pieces)

    def to_fsdp(f):
        return {"fsdp": f}

    barrier = pltpu.get_barrier_semaphore()

    def greet(device):
        pl.semaphore_signal(barrier, inc=1, device_id=device, device_id_type=MESH)

    greet(to_fsdp(other))
    for k in range(1, n_tp):
        greet({"tp": (t + k) % n_tp})
    pl.when(has_lo)(lambda: greet(to_fsdp(me - 2)))
    pl.when(has_hi)(lambda: greet(to_fsdp(me + 2)))

    def slot_of(e, lo, side):
        return (z - e if lo else z + e) * 2 + side

    bases = (base_o, base_d)
    helds = (held_o, held_d)

    def read(p, f):
        rows = pl.ds(pl.multiple_of(f * sizes[p], 16), sizes[p])
        return pltpu.make_async_copy(
            bases[p].at[:, rows], helds[p].at[:, rows], read_sem.at[p, f]
        )

    def read_slot(f):
        for p in range(2):
            read(p, f).start()

    read_slot(me)
    read_slot(other)

    @pl.loop(1, depth)
    def _(d):
        for side in (y, 1 - y):
            pl.when(z - d >= 0)(lambda: read_slot(slot_of(d, True, side)))
            pl.when(z + d < depth)(lambda: read_slot(slot_of(d, False, side)))

    def rows_of(c):
        p, first, rows = pieces[c]
        return pl.ds(starts[p] + first, rows)

    def fill(p):
        a = (a_o, a_d)[p]
        parts = []
        for layer in range(layers):
            rows = a[layer, :, 0, :].astype(F32)
            for u in range(1, n_tp):
                rows = jnp.where(t == u, a[layer, :, u, :].astype(F32), rows)
            parts.append(rows)
        block[pl.ds(starts[p], sizes[p]), :] = jnp.concatenate(parts, axis=0).T.astype(BF16)

    def send(source, f, c, way, target):
        return pltpu.make_async_remote_copy(
            src_ref=source.at[rows_of(c)],
            dst_ref=full_a.at[f, rows_of(c)],
            send_sem=send_sem.at[way, f],
            recv_sem=recv_sem.at[f, c],
            device_id=to_fsdp(target),
            device_id_type=MESH,
        )

    def arrived(f, c):
        send(full_a.at[f], f, c, 0, other).wait_recv()

    def own_sends(c):
        send(block, me, c, 0, other).start()
        pl.when(has_lo)(lambda: send(block, me, c, 1, me - 2).start())
        pl.when(has_hi)(lambda: send(block, me, c, 2, me + 2).start())

    def sent(f, way):
        pltpu.make_async_remote_copy(
            src_ref=block,
            dst_ref=full_a.at[f],
            send_sem=send_sem.at[way, f],
            recv_sem=recv_sem.at[f, 0],
            device_id=to_fsdp(other),
            device_id_type=MESH,
        ).wait_send()

    ends = has_lo.astype(jnp.int32) + has_hi.astype(jnp.int32)
    for p in range(2):
        fill(p)
        if p == 0:
            pl.semaphore_wait(barrier, n_tp + ends)
        for c in range(count):
            if pieces[c][0] == p:
                own_sends(c)

    full_a[me] = block[...]
    for p, b in enumerate((b_o, b_d)):
        for layer in range(layers):
            weights[p, layer] = jnp.zeros((layers * rank, columns), BF16)
            weights[p, layer, pl.ds(layer * rank, rank), :] = (
                b[layer].astype(F32) * 0.25
            ).astype(BF16)
    acc[...] = jnp.zeros_like(acc)

    wide = 256 if columns % 256 == 0 else columns

    def process(f, c):
        p, first, rows = pieces[c]
        left = full_a[f, rows_of(c), :]
        held = pl.ds(pl.multiple_of(f * sizes[p] + first, 16), rows)
        for layer in range(layers):
            for k in range(0, columns, wide):
                cut = pl.ds(k, wide)
                total = jnp.dot(
                    left, weights[p, layer, :, cut], preferred_element_type=F32
                ) + helds[p][layer, held, cut].astype(F32)
                acc[p, layer, :, cut] += jnp.sum(
                    (total * total).reshape(rows // 8, 8, wide), axis=0
                )

    def landed(f):
        for p in range(2):
            read(p, f).wait()

    def whole(f):
        landed(f)
        for c in range(count):
            process(f, c)

    def from_other(e):
        def take(f):
            landed(f)
            for c in range(count):
                arrived(f, c)
                process(f, c)

        pl.when(z - e >= 0)(lambda: take(slot_of(e, True, 1 - y)))
        pl.when((e > 0) & (z + e < depth))(lambda: take(slot_of(e, False, 1 - y)))

    whole(me)

    def relays(d):
        for c in range(count):

            @pl.when(z - d >= 0)
            def _():
                f = slot_of(d, True, y)
                arrived(f, c)
                pl.when(has_hi)(lambda: send(full_a.at[f], f, c, 2, me + 2).start())
                send(full_a.at[f], f, c, 0, other).start()

            @pl.when(z + d < depth)
            def _():
                f = slot_of(d, False, y)
                arrived(f, c)
                pl.when(has_lo)(lambda: send(full_a.at[f], f, c, 1, me - 2).start())
                send(full_a.at[f], f, c, 0, other).start()

    @pl.loop(1, depth)
    def _(d):
        relays(d)
        from_other(d - 1)
        pl.when(z - d >= 0)(lambda: whole(slot_of(d, True, y)))
        pl.when(z + d < depth)(lambda: whole(slot_of(d, False, y)))

    from_other(jnp.int32(depth - 1))

    for p in range(2):
        for layer in range(layers):
            sums[p * layers + layer, :] = jnp.sum(acc[p, layer], axis=0)

    def share(k):
        return pltpu.make_async_remote_copy(
            src_ref=sums,
            dst_ref=peers.at[k - 1],
            send_sem=sum_send.at[k - 1],
            recv_sem=sum_recv.at[k - 1],
            device_id={"tp": (t + k) % n_tp},
            device_id_type=MESH,
        )

    for k in range(1, n_tp):
        share(k).start()

    sent(me, 0)
    pl.when(has_lo)(lambda: sent(me, 1))
    pl.when(has_hi)(lambda: sent(me, 2))

    @pl.loop(1, depth)
    def _(d):
        @pl.when(z - d >= 0)
        def _():
            f = slot_of(d, True, y)
            pl.when(has_hi)(lambda: sent(f, 2))
            sent(f, 0)

        @pl.when(z + d < depth)
        def _():
            f = slot_of(d, False, y)
            pl.when(has_lo)(lambda: sent(f, 1))
            sent(f, 0)

    square = sums[...]
    for k in range(1, n_tp):
        share(k).wait()
    for k in range(1, n_tp):
        square = square + peers[k - 1]
    magnitude = jnp.concatenate([mag_o[...], mag_d[...]], axis=0)
    scale[...] = magnitude * lax.rsqrt(square + 1e-06)


def finish_kernel(
    n, sizes, held_o, held_d, full_a, weights, scale, out_o, out_d, made_o, made_d, sem
):
    layers, _, columns = held_o.shape
    slots = made_o.shape[0]
    wide = 256 if columns % 256 == 0 else columns
    trio = ((held_o, out_o, made_o), (held_d, out_d, made_d))

    def write(p, i):
        _, out, made = trio[p]
        rows = pl.ds(pl.multiple_of((i % n) * sizes[p], 16), sizes[p])
        return pltpu.make_async_copy(
            made.at[i % slots], out.at[i // n, rows], sem.at[p, i % slots]
        )

    @pl.loop(0, layers * n)
    def _(i):
        layer, f = i // n, i % n

        @pl.when(i >= slots)
        def _():
            for p in range(2):
                write(p, i - slots).wait()

        for p, (held, _, made) in enumerate(trio):
            size, start = sizes[p], sum(sizes[:p])
            factor = scale[pl.ds(p * layers + layer, 1), :]
            left = full_a[f, pl.ds(start, size), :]
            inside = pl.ds(pl.multiple_of(f * size, 16), size)
            for c in range(0, columns, wide):
                cut = pl.ds(c, wide)
                total = jnp.dot(
                    left, weights[p, layer, :, cut], preferred_element_type=F32
                ) + held[layer, inside, cut].astype(F32)
                made[i % slots, :, cut] = (total * factor[:, c : c + wide]).astype(BF16)
        for p in range(2):
            write(p, i).start()

    @pl.loop(layers * n - slots, layers * n)
    def _(i):
        for p in range(2):
            write(p, i).wait()


def solution(mesh):
    n, n_tp = mesh.shape["fsdp"], mesh.shape["tp"]
    in_vmem = pl.BlockSpec(memory_space=pltpu.VMEM)
    anywhere = pl.BlockSpec(memory_space=pl.ANY)

    def local(base_o, base_d, a_o, b_o, a_d, b_d, mag_o, mag_d):
        layers, rank, _, part_o = a_o.shape
        sizes = (part_o, a_d.shape[3])
        columns = base_o.shape[2]
        depth = layers * rank
        count = len(pieces_of(sizes, 448))
        base_o = pltpu.with_memory_space_constraint(base_o, pltpu.HBM)
        base_d = pltpu.with_memory_space_constraint(base_d, pltpu.HBM)
        shapes = (
            pltpu.VMEM(base_o.shape, BF16),
            pltpu.VMEM(base_d.shape, BF16),
            pltpu.VMEM((n, sum(sizes), depth), BF16),
            pltpu.VMEM((2, layers, depth, columns), BF16),
            pltpu.VMEM((2 * layers, columns), F32),
        )
        held_o, held_d, full_a, weights, scale = pl.pallas_call(
            functools.partial(gather_kernel, n, n_tp, sizes, rank),
            out_shape=shapes,
            in_specs=[anywhere] * 2 + [in_vmem] * 6,
            out_specs=[in_vmem] * 5,
            scratch_shapes=[
                pltpu.VMEM((sum(sizes), depth), BF16),
                pltpu.VMEM((2, layers, 8, columns), F32),
                pltpu.VMEM((2 * layers, columns), F32),
                pltpu.VMEM((n_tp - 1, 2 * layers, columns), F32),
                pltpu.SemaphoreType.DMA((2, n)),
                pltpu.SemaphoreType.DMA((3, n)),
                pltpu.SemaphoreType.DMA((n, count)),
                pltpu.SemaphoreType.DMA((n_tp - 1,)),
                pltpu.SemaphoreType.DMA((n_tp - 1,)),
            ],
            compiler_params=pltpu.CompilerParams(
                collective_id=0, has_side_effects=True, vmem_limit_bytes=20 << 20
            ),
            name="gather_squares",
        )(
            base_o, base_d, a_o, a_d, b_o.swapaxes(1, 2), b_d.swapaxes(1, 2), mag_o, mag_d
        )

        kept = [
            pltpu.with_memory_space_constraint(x, pltpu.VMEM)
            for x in (held_o, held_d, full_a, weights, scale)
        ]
        return pl.pallas_call(
            functools.partial(finish_kernel, n, sizes),
            out_shape=[jax.ShapeDtypeStruct(b.shape, BF16) for b in (base_o, base_d)],
            in_specs=[in_vmem] * 5,
            out_specs=[pl.BlockSpec(memory_space=pltpu.HBM)] * 2,
            scratch_shapes=[pltpu.VMEM((4, size, columns), BF16) for size in sizes]
            + [pltpu.SemaphoreType.DMA((2, 4))],
            compiler_params=pltpu.CompilerParams(vmem_limit_bytes=20 << 20),
            name="finish",
        )(*kept)

    return jax.shard_map(
        local,
        mesh=mesh,
        in_specs=(
            P(None, "tp", "fsdp"),
            P(None, "tp", "fsdp"),
            P(None, None, None, "fsdp"),
            P(None, "fsdp", None),
            P(None, None, None, "fsdp"),
            P(None, "fsdp", None),
            P(None, "fsdp"),
            P(None, "fsdp"),
        ),
        out_specs=(P(None, "tp", "fsdp"), P(None, "tp", "fsdp")),
        check_vma=False,
    )
```

time: 66.8 us -> 50.8 us (0.76)
  Pallas kernels: 66 us -> 50 us
    pallas_call x1, Pallas kernels: 23.5 us -> 13.7 us  [local(): pl.pallas_call(functools.partial(finish_kernel, n, sizes), out_shape=[jax...]
    pallas_call x1, Pallas kernels: 42.5 us -> 36.3 us  [local(): pl.pallas_call(functools.partial(gather_kernel, n, n_tp, sizes, rank), ou...]
where the time goes in v1:
time: 50.8 us; the launch traced here: 50.6 us
  Pallas kernels  50 us (98%)
  between operations  0.64 us (1%)
    pallas_call x1, Pallas kernels, local(): pl.pallas_call(functools.partial(gather_kernel, n, n_tp, sizes, rank), ou...  36.3 us
    pallas_call x1, Pallas kernels, local(): pl.pallas_call(functools.partial(finish_kernel, n, sizes), out_shape=[jax...  13.7 us

profile of v1, /device:TPU:0, one launch (start us, length us, event | category | flops | bytes accessed | tf_op | source)
XLA Modules:
  0.0 50.6 jit_solution(1795058745501392029)
XLA Ops:
  0.6 36.3 %gather_squares.1 = (bf16[2,2048,1024]{2,1,0:T(8,128)(2,1)S(1)}, bf16[2,7168,1024]{2,1,0:T(8,128)(2,1)S(1)}, bf16[8,1152,128]{2,1,0:T(8,128)(2,1)S(1)}, bf16[2,2...) custom-call(bf16[2,2048,1024]{2,1,0:T(8,128)(2,1)} %base_o.1, bf16[2,7168,1024]{2,1,0:T(8,128)(2,1)} %base_d.1, ...), custom_call_target="tpu_custom_call" | custom-call | tf_op jit(solution)/shard_map/gather_squares/pallas_call | solution.py:331
  36.9 13.7 %finish.1 = (bf16[2,2048,1024]{2,1,0:T(8,128)(2,1)}, bf16[2,7168,1024]{2,1,0:T(8,128)(2,1)}) custom-call(bf16[2,2048,1024]{2,1,0:T(8,128)(2,1)S(1)} %get-tuple-element.7.held_o, bf16[2,7168,1024]{2,1,0:T(8,128)(2,1)S(1)} %get-tuple-element.8.held_d, bf16[8,1152,128]{2,1,0:T(8,128)(2,1)S(1)} %get-tuple-element.9.full_a, ...), custom_call_target="tpu_custom_call" | custom-call | tf_op jit(solution)/shard_map/finish/pallas_call | solution.py:359

commit v2 on v1

--- a/solution.py
+++ b/solution.py
@@ -10,14 +10,14 @@
 MESH = pl.DeviceIdType.MESH
 F32 = jnp.float32
 BF16 = jnp.bfloat16
-
-
-def pieces_of(sizes, most):
-    found = []
-    for p, size in enumerate(sizes):
-        rows = max(t for t in range(16, most + 1, 16) if size % t == 0)
-        found += [(p, k * rows, rows) for k in range(size // rows)]
-    return found
+LAST = 96
+
+
+def pieces_of(sizes):
+    last = sum(sizes) // LAST * 16
+    late = sum(sizes) // 32 * 16
+    early = sizes[1] - late
+    return [(0, 0, sizes[0]), (1, 0, early), (1, early, late - last), (1, sizes[1] - last, last)]
 
 
 def gather_kernel(
@@ -42,6 +42,12 @@
     acc,
     sums,
     peers,
+    kept_a_o,
+    kept_a_d,
+    kept_b_o,
+    kept_b_d,
+    kept_mag,
+    load_sem,
     read_sem,
     send_sem,
     recv_sem,
@@ -55,8 +61,11 @@
     other = z * 2 + 1 - y
     has_lo, has_hi = z > 0, z < depth - 1
     starts = (0, sizes[0])
-    pieces = pieces_of(sizes, 448)
+    pieces = pieces_of(sizes)
     count = len(pieces)
+    early, late = range(count - 2), range(count - 2, count)
+    cut_row = starts[1] + pieces[count - 2][1]
+    mate = (z + 1 - 2 * (z % 2)) * 2
 
     def to_fsdp(f):
         return {"fsdp": f}
@@ -72,6 +81,22 @@
     pl.when(has_lo)(lambda: greet(to_fsdp(me - 2)))
     pl.when(has_hi)(lambda: greet(to_fsdp(me + 2)))
 
+    loads = [
+        pltpu.make_async_copy(source, target, load_sem.at[k])
+        for k, (source, target) in enumerate(
+            (
+                (a_o, kept_a_o),
+                (a_d, kept_a_d),
+                (b_o, kept_b_o),
+                (b_d, kept_b_d),
+                (mag_o, kept_mag.at[0]),
+                (mag_d, kept_mag.at[1]),
+            )
+        )
+    ]
+    for load in loads:
+        load.start()
+
     def slot_of(e, lo, side):
         return (z - e if lo else z + e) * 2 + side
 
@@ -102,7 +127,8 @@
         return pl.ds(starts[p] + first, rows)
 
     def fill(p):
-        a = (a_o, a_d)[p]
+        a = (kept_a_o, kept_a_d)[p]
+        loads[p].wait()
         parts = []
         for layer in range(layers):
             rows = a[layer, :, 0, :].astype(F32)
@@ -129,10 +155,10 @@
         pl.when(has_lo)(lambda: send(block, me, c, 1, me - 2).start())
         pl.when(has_hi)(lambda: send(block, me, c, 2, me + 2).start())
 
-    def sent(f, way):
+    def sent(f, way, rows):
         pltpu.make_async_remote_copy(
-            src_ref=block,
-            dst_ref=full_a.at[f],
+            src_ref=block.at[rows],
+            dst_ref=full_a.at[f, rows],
             send_sem=send_sem.at[way, f],
             recv_sem=recv_sem.at[f, 0],
             device_id=to_fsdp(other),
@@ -149,7 +175,8 @@
                 own_sends(c)
 
     full_a[me] = block[...]
-    for p, b in enumerate((b_o, b_d)):
+    for p, b in enumerate((kept_b_o, kept_b_d)):
+        loads[2 + p].wait()
         for layer in range(layers):
             weights[p, layer] = jnp.zeros((layers * rank, columns), BF16)
             weights[p, layer, pl.ds(layer * rank, rank), :] = (
@@ -177,48 +204,56 @@
         for p in range(2):
             read(p, f).wait()
 
-    def whole(f):
-        landed(f)
+    def own_column(f, c):
+        if c == 0:
+            landed(f)
+        process(f, c)
+
+    def take(f, c):
+        arrived(f, c)
+        process(f, c)
+
+    def other_column(f, c):
+        if c == 0:
+            landed(f)
+        if c in early:
+            take(f, c)
+        else:
+            pl.when(f != mate + 1 - y)(lambda: take(f, c))
+
+    for c in range(count):
+        own_column(me, c)
+
+    def relay(f, c, way, more, target):
+        arrived(f, c)
+        pl.when(more)(lambda: send(full_a.at[f], f, c, way, target).start())
+        if c in early:
+            send(full_a.at[f], f, c, 0, other).start()
+        else:
+            pl.when(f != mate + y)(lambda: send(full_a.at[f], f, c, 0, other).start())
+
+    def cross(act):
+        pl.when(z % 2 == 1)(lambda: act(1, me - 2))
+        pl.when(z % 2 == 0)(lambda: act(2, me + 2))
+
+    def start_cross(way, target):
+        for c in late:
+            send(full_a.at[other], other, c, way, target).start()
+
+    @pl.loop(1, depth + 1)
+    def _(d):
+        pl.when(d == max(depth - 1, 1))(lambda: cross(start_cross))
         for c in range(count):
-            process(f, c)
-
-    def from_other(e):
-        def take(f):
-            landed(f)
-            for c in range(count):
-                arrived(f, c)
-                process(f, c)
-
-        pl.when(z - e >= 0)(lambda: take(slot_of(e, True, 1 - y)))
-        pl.when((e > 0) & (z + e < depth))(lambda: take(slot_of(e, False, 1 - y)))
-
-    whole(me)
-
-    def relays(d):
-        for c in range(count):
-
-            @pl.when(z - d >= 0)
-            def _():
-                f = slot_of(d, True, y)
-                arrived(f, c)
-                pl.when(has_hi)(lambda: send(full_a.at[f], f, c, 2, me + 2).start())
-                send(full_a.at[f], f, c, 0, other).start()
-
-            @pl.when(z + d < depth)
-            def _():
-                f = slot_of(d, False, y)
-                arrived(f, c)
-                pl.when(has_lo)(lambda: send(full_a.at[f], f, c, 1, me - 2).start())
-                send(full_a.at[f], f, c, 0, other).start()
-
-    @pl.loop(1, depth)
-    def _(d):
-        relays(d)
-        from_other(d - 1)
-        pl.when(z - d >= 0)(lambda: whole(slot_of(d, True, y)))
-        pl.when(z + d < depth)(lambda: whole(slot_of(d, False, y)))
-
-    from_other(jnp.int32(depth - 1))
+            pl.when(z - d >= 0)(lambda: relay(slot_of(d, True, y), c, 2, has_hi, me + 2))
+            pl.when(z + d < depth)(lambda: relay(slot_of(d, False, y), c, 1, has_lo, me - 2))
+            if c in late:
+                pl.when(d == depth)(lambda: take(mate + 1 - y, c))
+            pl.when(z - d + 1 >= 0)(lambda: other_column(slot_of(d - 1, True, 1 - y), c))
+            pl.when((d > 1) & (z + d - 1 < depth))(
+                lambda: other_column(slot_of(d - 1, False, 1 - y), c)
+            )
+            pl.when(z - d >= 0)(lambda: own_column(slot_of(d, True, y), c))
+            pl.when(z + d < depth)(lambda: own_column(slot_of(d, False, y), c))
 
     for p in range(2):
         for layer in range(layers):
@@ -237,30 +272,31 @@
     for k in range(1, n_tp):
         share(k).start()
 
-    sent(me, 0)
-    pl.when(has_lo)(lambda: sent(me, 1))
-    pl.when(has_hi)(lambda: sent(me, 2))
+    every = pl.ds(0, sum(sizes))
+    first, rest = pl.ds(0, cut_row), pl.ds(cut_row, sum(sizes) - cut_row)
+    sent(me, 0, every)
+    pl.when(has_lo)(lambda: sent(me, 1, every))
+    pl.when(has_hi)(lambda: sent(me, 2, every))
+    sent(mate + y, 0, first)
+    cross(lambda way, _: sent(other, way, rest))
+
+    def relayed(f, way, more):
+        pl.when(more)(lambda: sent(f, way, every))
+        pl.when(f != mate + y)(lambda: sent(f, 0, every))
 
     @pl.loop(1, depth)
     def _(d):
-        @pl.when(z - d >= 0)
-        def _():
-            f = slot_of(d, True, y)
-            pl.when(has_hi)(lambda: sent(f, 2))
-            sent(f, 0)
-
-        @pl.when(z + d < depth)
-        def _():
-            f = slot_of(d, False, y)
-            pl.when(has_lo)(lambda: sent(f, 1))
-            sent(f, 0)
+        pl.when(z - d >= 0)(lambda: relayed(slot_of(d, True, y), 2, has_hi))
+        pl.when(z + d < depth)(lambda: relayed(slot_of(d, False, y), 1, has_lo))
 
     square = sums[...]
     for k in range(1, n_tp):
         share(k).wait()
     for k in range(1, n_tp):
         square = square + peers[k - 1]
-    magnitude = jnp.concatenate([mag_o[...], mag_d[...]], axis=0)
+    loads[4].wait()
+    loads[5].wait()
+    magnitude = jnp.concatenate([kept_mag[0], kept_mag[1]], axis=0)
     scale[...] = magnitude * lax.rsqrt(square + 1e-06)
 
 
@@ -272,40 +308,43 @@
     wide = 256 if columns % 256 == 0 else columns
     trio = ((held_o, out_o, made_o), (held_d, out_d, made_d))
 
-    def write(p, i):
+    turns = slots // layers
+
+    def write(p, layer, f):
         _, out, made = trio[p]
-        rows = pl.ds(pl.multiple_of((i % n) * sizes[p], 16), sizes[p])
-        return pltpu.make_async_copy(
-            made.at[i % slots], out.at[i // n, rows], sem.at[p, i % slots]
-        )
-
-    @pl.loop(0, layers * n)
-    def _(i):
-        layer, f = i // n, i % n
-
-        @pl.when(i >= slots)
+        rows = pl.ds(pl.multiple_of(f * sizes[p], 16), sizes[p])
+        slot = (f % turns) * layers + layer
+        return pltpu.make_async_copy(made.at[slot], out.at[layer, rows], sem.at[p, slot])
+
+    @pl.loop(0, n)
+    def _(f):
+        @pl.when(f >= turns)
         def _():
+            for layer in range(layers):
+                for p in range(2):
+                    write(p, layer, f - turns).wait()
+
+        for layer in range(layers):
+            for p, (held, _, made) in enumerate(trio):
+                size, start = sizes[p], sum(sizes[:p])
+                factor = scale[pl.ds(p * layers + layer, 1), :]
+                left = full_a[f, pl.ds(start, size), :]
+                inside = pl.ds(pl.multiple_of(f * size, 16), size)
+                for c in range(0, columns, wide):
+                    cut = pl.ds(c, wide)
+                    total = jnp.dot(
+                        left, weights[p, layer, :, cut], preferred_element_type=F32
+                    ) + held[layer, inside, cut].astype(F32)
+                    made[(f % turns) * layers + layer, :, cut] = (
+                        total * factor[:, c : c + wide]
+                    ).astype(BF16)
+                write(p, layer, f).start()
+
+    @pl.loop(n - turns, n)
+    def _(f):
+        for layer in range(layers):
             for p in range(2):
-                write(p, i - slots).wait()
-
-        for p, (held, _, made) in enumerate(trio):
-            size, start = sizes[p], sum(sizes[:p])
-            factor = scale[pl.ds(p * layers + layer, 1), :]
-            left = full_a[f, pl.ds(start, size), :]
-            inside = pl.ds(pl.multiple_of(f * size, 16), size)
-            for c in range(0, columns, wide):
-                cut = pl.ds(c, wide)
-                total = jnp.dot(
-                    left, weights[p, layer, :, cut], preferred_element_type=F32
-                ) + held[layer, inside, cut].astype(F32)
-                made[i % slots, :, cut] = (total * factor[:, c : c + wide]).astype(BF16)
-        for p in range(2):
-            write(p, i).start()
-
-    @pl.loop(layers * n - slots, layers * n)
-    def _(i):
-        for p in range(2):
-            write(p, i).wait()
+                write(p, layer, f).wait()
 
 
 def solution(mesh):
@@ -318,9 +357,12 @@
         sizes = (part_o, a_d.shape[3])
         columns = base_o.shape[2]
         depth = layers * rank
-        count = len(pieces_of(sizes, 448))
-        base_o = pltpu.with_memory_space_constraint(base_o, pltpu.HBM)
-        base_d = pltpu.with_memory_space_constraint(base_d, pltpu.HBM)
+        count = len(pieces_of(sizes))
+        b_o, b_d = b_o.swapaxes(1, 2), b_d.swapaxes(1, 2)
+        given = [
+            pltpu.with_memory_space_constraint(x, pltpu.HBM)
+            for x in (base_o, base_d, a_o, a_d, b_o, b_d, mag_o, mag_d)
+        ]
         shapes = (
             pltpu.VMEM(base_o.shape, BF16),
             pltpu.VMEM(base_d.shape, BF16),
@@ -331,13 +373,19 @@
         held_o, held_d, full_a, weights, scale = pl.pallas_call(
             functools.partial(gather_kernel, n, n_tp, sizes, rank),
             out_shape=shapes,
-            in_specs=[anywhere] * 2 + [in_vmem] * 6,
+            in_specs=[anywhere] * 8,
             out_specs=[in_vmem] * 5,
             scratch_shapes=[
                 pltpu.VMEM((sum(sizes), depth), BF16),
                 pltpu.VMEM((2, layers, 8, columns), F32),
                 pltpu.VMEM((2 * layers, columns), F32),
                 pltpu.VMEM((n_tp - 1, 2 * layers, columns), F32),
+                pltpu.VMEM(a_o.shape, BF16),
+                pltpu.VMEM(a_d.shape, BF16),
+                pltpu.VMEM(b_o.shape, BF16),
+                pltpu.VMEM(b_d.shape, BF16),
+                pltpu.VMEM((2, layers, columns), F32),
+                pltpu.SemaphoreType.DMA((6,)),
                 pltpu.SemaphoreType.DMA((2, n)),
                 pltpu.SemaphoreType.DMA((3, n)),
                 pltpu.SemaphoreType.DMA((n, count)),
@@ -348,9 +396,7 @@
                 collective_id=0, has_side_effects=True, vmem_limit_bytes=20 << 20
             ),
             name="gather_squares",
-        )(
-            base_o, base_d, a_o, a_d, b_o.swapaxes(1, 2), b_d.swapaxes(1, 2), mag_o, mag_d
-        )
+        )(*given)
 
         kept = [
             pltpu.with_memory_space_constraint(x, pltpu.VMEM)

time: 50.8 us -> 47.4 us (0.933)
  Pallas kernels: 50 us -> 46.7 us
    pallas_call x1, Pallas kernels: 36.3 us -> 33.8 us  [local(): pl.pallas_call(functools.partial(gather_kernel, n, n_tp, sizes, rank), ou...]
    pallas_call x1, Pallas kernels: 13.7 us -> 12.8 us  [local(): pl.pallas_call(functools.partial(finish_kernel, n, sizes), out_shape=[jax...]
where the time goes in v2:
time: 47.4 us; the launch traced here: 47.3 us
  Pallas kernels  46.7 us (99%)
  between operations  0.64 us (1%)
    pallas_call x1, Pallas kernels, local(): pl.pallas_call(functools.partial(gather_kernel, n, n_tp, sizes, rank), ou...  33.8 us
    pallas_call x1, Pallas kernels, local(): pl.pallas_call(functools.partial(finish_kernel, n, sizes), out_shape=[jax...  12.8 us

profile of v2, /device:TPU:0, one launch (start us, length us, event | category | flops | bytes accessed | tf_op | source)
XLA Modules:
  0.0 47.3 jit_solution(10044833328765225006)
XLA Ops:
  0.6 33.8 %gather_squares.1 = (bf16[2,2048,1024]{2,1,0:T(8,128)(2,1)S(1)}, bf16[2,7168,1024]{2,1,0:T(8,128)(2,1)S(1)}, bf16[8,1152,128]{2,1,0:T(8,128)(2,1)S(1)}, bf16[2,2...) custom-call(bf16[2,2048,1024]{2,1,0:T(8,128)(2,1)} %base_o.1, bf16[2,7168,1024]{2,1,0:T(8,128)(2,1)} %base_d.1, ...), custom_call_target="tpu_custom_call" | custom-call | tf_op jit(solution)/shard_map/gather_squares/pallas_call | solution.py:373
  34.5 12.8 %finish.1 = (bf16[2,2048,1024]{2,1,0:T(8,128)(2,1)}, bf16[2,7168,1024]{2,1,0:T(8,128)(2,1)}) custom-call(bf16[2,2048,1024]{2,1,0:T(8,128)(2,1)S(1)} %get-tuple-element.7.held_o, bf16[2,7168,1024]{2,1,0:T(8,128)(2,1)S(1)} %get-tuple-element.8.held_d, bf16[8,1152,128]{2,1,0:T(8,128)(2,1)S(1)} %get-tuple-element.9.full_a, ...), custom_call_target="tpu_custom_call" | custom-call | tf_op jit(solution)/shard_map/finish/pallas_call | solution.py:405

commit v3 on v2

--- a/solution.py
+++ b/solution.py
@@ -64,7 +64,6 @@
     pieces = pieces_of(sizes)
     count = len(pieces)
     early, late = range(count - 2), range(count - 2, count)
-    cut_row = starts[1] + pieces[count - 2][1]
     mate = (z + 1 - 2 * (z % 2)) * 2
 
     def to_fsdp(f):
@@ -106,7 +105,7 @@
     def read(p, f):
         rows = pl.ds(pl.multiple_of(f * sizes[p], 16), sizes[p])
         return pltpu.make_async_copy(
-            bases[p].at[:, rows], helds[p].at[:, rows], read_sem.at[p, f]
+            bases[p].at[:, rows], helds[p].at[:, rows], read_sem.at[f]
         )
 
     def read_slot(f):
@@ -137,11 +136,11 @@
             parts.append(rows)
         block[pl.ds(starts[p], sizes[p]), :] = jnp.concatenate(parts, axis=0).T.astype(BF16)
 
-    def send(source, f, c, way, target):
+    def send(source, f, c, lane, target):
         return pltpu.make_async_remote_copy(
             src_ref=source.at[rows_of(c)],
             dst_ref=full_a.at[f, rows_of(c)],
-            send_sem=send_sem.at[way, f],
+            send_sem=send_sem.at[lane],
             recv_sem=recv_sem.at[f, c],
             device_id=to_fsdp(target),
             device_id_type=MESH,
@@ -153,14 +152,15 @@
     def own_sends(c):
         send(block, me, c, 0, other).start()
         pl.when(has_lo)(lambda: send(block, me, c, 1, me - 2).start())
-        pl.when(has_hi)(lambda: send(block, me, c, 2, me + 2).start())
-
-    def sent(f, way, rows):
+        pl.when(has_hi)(lambda: send(block, me, c, 1, me + 2).start())
+
+    def sent(lane, blocks):
+        whole = full_a.at[pl.ds(0, blocks)]
         pltpu.make_async_remote_copy(
-            src_ref=block.at[rows],
-            dst_ref=full_a.at[f, rows],
-            send_sem=send_sem.at[way, f],
-            recv_sem=recv_sem.at[f, 0],
+            src_ref=whole,
+            dst_ref=whole,
+            send_sem=send_sem.at[lane],
+            recv_sem=recv_sem.at[0, 0],
             device_id=to_fsdp(other),
             device_id_type=MESH,
         ).wait_send()
@@ -201,8 +201,8 @@
                 )
 
     def landed(f):
-        for p in range(2):
-            read(p, f).wait()
+        rows = pl.ds(0, sum(sizes))
+        pltpu.make_async_copy(base_d.at[:, rows], held_d.at[:, rows], read_sem.at[f]).wait()
 
     def own_column(f, c):
         if c == 0:
@@ -224,28 +224,49 @@
     for c in range(count):
         own_column(me, c)
 
-    def relay(f, c, way, more, target):
+    def relay(f, c, more, target):
         arrived(f, c)
-        pl.when(more)(lambda: send(full_a.at[f], f, c, way, target).start())
+        pl.when(more)(lambda: send(full_a.at[f], f, c, 1, target).start())
         if c in early:
             send(full_a.at[f], f, c, 0, other).start()
         else:
             pl.when(f != mate + y)(lambda: send(full_a.at[f], f, c, 0, other).start())
 
     def cross(act):
-        pl.when(z % 2 == 1)(lambda: act(1, me - 2))
-        pl.when(z % 2 == 0)(lambda: act(2, me + 2))
-
-    def start_cross(way, target):
+        pl.when(z % 2 == 1)(lambda: act(me - 2))
+        pl.when(z % 2 == 0)(lambda: act(me + 2))
+
+    def start_cross(target):
         for c in late:
-            send(full_a.at[other], other, c, way, target).start()
+            send(full_a.at[other], other, c, 0, target).start()
+
+    def share(k, p):
+        return pltpu.make_async_remote_copy(
+            src_ref=sums.at[p],
+            dst_ref=peers.at[k - 1, p],
+            send_sem=sum_send.at[k - 1, p],
+            recv_sem=sum_recv.at[k - 1, p],
+            device_id={"tp": (t + k) % n_tp},
+            device_id_type=MESH,
+        )
+
+    def share_sums(p):
+        for layer in range(layers):
+            sums[p, layer, :] = jnp.sum(acc[p, layer], axis=0)
+        for k in range(1, n_tp):
+            share(k, p).start()
 
     @pl.loop(1, depth + 1)
     def _(d):
         pl.when(d == max(depth - 1, 1))(lambda: cross(start_cross))
+        def relays(c):
+            pl.when(z + d < depth)(lambda: relay(slot_of(d, False, y), c, has_lo, me - 2))
+            pl.when(z - d >= 0)(lambda: relay(slot_of(d, True, y), c, has_hi, me + 2))
+
+        relays(0)
         for c in range(count):
-            pl.when(z - d >= 0)(lambda: relay(slot_of(d, True, y), c, 2, has_hi, me + 2))
-            pl.when(z + d < depth)(lambda: relay(slot_of(d, False, y), c, 1, has_lo, me - 2))
+            if c + 1 < count:
+                relays(c + 1)
             if c in late:
                 pl.when(d == depth)(lambda: take(mate + 1 - y, c))
             pl.when(z - d + 1 >= 0)(lambda: other_column(slot_of(d - 1, True, 1 - y), c))
@@ -254,50 +275,23 @@
             )
             pl.when(z - d >= 0)(lambda: own_column(slot_of(d, True, y), c))
             pl.when(z + d < depth)(lambda: own_column(slot_of(d, False, y), c))
-
-    for p in range(2):
-        for layer in range(layers):
-            sums[p * layers + layer, :] = jnp.sum(acc[p, layer], axis=0)
-
-    def share(k):
-        return pltpu.make_async_remote_copy(
-            src_ref=sums,
-            dst_ref=peers.at[k - 1],
-            send_sem=sum_send.at[k - 1],
-            recv_sem=sum_recv.at[k - 1],
-            device_id={"tp": (t + k) % n_tp},
-            device_id_type=MESH,
-        )
-
-    for k in range(1, n_tp):
-        share(k).start()
-
-    every = pl.ds(0, sum(sizes))
-    first, rest = pl.ds(0, cut_row), pl.ds(cut_row, sum(sizes) - cut_row)
-    sent(me, 0, every)
-    pl.when(has_lo)(lambda: sent(me, 1, every))
-    pl.when(has_hi)(lambda: sent(me, 2, every))
-    sent(mate + y, 0, first)
-    cross(lambda way, _: sent(other, way, rest))
-
-    def relayed(f, way, more):
-        pl.when(more)(lambda: sent(f, way, every))
-        pl.when(f != mate + y)(lambda: sent(f, 0, every))
-
-    @pl.loop(1, depth)
-    def _(d):
-        pl.when(z - d >= 0)(lambda: relayed(slot_of(d, True, y), 2, has_hi))
-        pl.when(z + d < depth)(lambda: relayed(slot_of(d, False, y), 1, has_lo))
-
-    square = sums[...]
-    for k in range(1, n_tp):
-        share(k).wait()
-    for k in range(1, n_tp):
-        square = square + peers[k - 1]
+            if c == 0:
+                pl.when(d == depth)(lambda: share_sums(0))
+
+    share_sums(1)
+    sent(0, depth)
+    pl.when(has_lo & has_hi)(lambda: sent(1, depth + 1))
+    pl.when(~(has_lo & has_hi))(lambda: sent(1, 1))
+
     loads[4].wait()
     loads[5].wait()
-    magnitude = jnp.concatenate([kept_mag[0], kept_mag[1]], axis=0)
-    scale[...] = magnitude * lax.rsqrt(square + 1e-06)
+    for p in range(2):
+        square = sums[p]
+        for k in range(1, n_tp):
+            share(k, p).wait()
+        for k in range(1, n_tp):
+            square = square + peers[k - 1, p]
+        scale[pl.ds(p * layers, layers), :] = kept_mag[p] * lax.rsqrt(square + 1e-06)
 
 
 def finish_kernel(
@@ -378,19 +372,19 @@
             scratch_shapes=[
                 pltpu.VMEM((sum(sizes), depth), BF16),
                 pltpu.VMEM((2, layers, 8, columns), F32),
-                pltpu.VMEM((2 * layers, columns), F32),
-                pltpu.VMEM((n_tp - 1, 2 * layers, columns), F32),
+                pltpu.VMEM((2, layers, columns), F32),
+                pltpu.VMEM((n_tp - 1, 2, layers, columns), F32),
                 pltpu.VMEM(a_o.shape, BF16),
                 pltpu.VMEM(a_d.shape, BF16),
                 pltpu.VMEM(b_o.shape, BF16),
                 pltpu.VMEM(b_d.shape, BF16),
                 pltpu.VMEM((2, layers, columns), F32),
                 pltpu.SemaphoreType.DMA((6,)),
-                pltpu.SemaphoreType.DMA((2, n)),
-                pltpu.SemaphoreType.DMA((3, n)),
+                pltpu.SemaphoreType.DMA((n,)),
+                pltpu.SemaphoreType.DMA((2,)),
                 pltpu.SemaphoreType.DMA((n, count)),
-                pltpu.SemaphoreType.DMA((n_tp - 1,)),
-                pltpu.SemaphoreType.DMA((n_tp - 1,)),
+                pltpu.SemaphoreType.DMA((n_tp - 1, 2)),
+                pltpu.SemaphoreType.DMA((n_tp - 1, 2)),
             ],
             compiler_params=pltpu.CompilerParams(
                 collective_id=0, has_side_effects=True, vmem_limit_bytes=20 << 20

time: 47.4 us -> 47.1 us (level)
  no operation moved by 1% of the time
where the time goes in v3:
time: 47.1 us; the launch traced here: 47 us
  Pallas kernels  46.4 us (99%)
  between operations  0.64 us (1%)
    pallas_call x1, Pallas kernels, local(): pl.pallas_call(functools.partial(gather_kernel, n, n_tp, sizes, rank), ou...  33.5 us
    pallas_call x1, Pallas kernels, local(): pl.pallas_call(functools.partial(finish_kernel, n, sizes), out_shape=[jax...  12.8 us

profile of v3, /device:TPU:0, one launch (start us, length us, event | category | flops | bytes accessed | tf_op | source)
XLA Modules:
  0.0 47.0 jit_solution(10897296006061431184)
XLA Ops:
  0.6 33.5 %gather_squares.1 = (bf16[2,2048,1024]{2,1,0:T(8,128)(2,1)S(1)}, bf16[2,7168,1024]{2,1,0:T(8,128)(2,1)S(1)}, bf16[8,1152,128]{2,1,0:T(8,128)(2,1)S(1)}, bf16[2,2...) custom-call(bf16[2,2048,1024]{2,1,0:T(8,128)(2,1)} %base_o.1, bf16[2,7168,1024]{2,1,0:T(8,128)(2,1)} %base_d.1, ...), custom_call_target="tpu_custom_call" | custom-call | tf_op jit(solution)/shard_map/gather_squares/pallas_call | solution.py:367
  34.2 12.8 %finish.1 = (bf16[2,2048,1024]{2,1,0:T(8,128)(2,1)}, bf16[2,7168,1024]{2,1,0:T(8,128)(2,1)}) custom-call(bf16[2,2048,1024]{2,1,0:T(8,128)(2,1)S(1)} %get-tuple-element.7.held_o, bf16[2,7168,1024]{2,1,0:T(8,128)(2,1)S(1)} %get-tuple-element.8.held_d, bf16[8,1152,128]{2,1,0:T(8,128)(2,1)S(1)} %get-tuple-element.9.full_a, ...), custom_call_target="tpu_custom_call" | custom-call | tf_op jit(solution)/shard_map/finish/pallas_call | solution.py:399
